TPU v7x, 32 devices: a whole 2x2x4 slice. The times are simulated.
32 devices in a mesh: dp: 8 (over z, x), expert: 4 (over y, core).
Axes of the slice: x: 2, y: 2, z: 4, core: 2. Of those that a mesh axis runs over, the one named last changes fastest.
Arguments:
- tokens: bfloat16 [4096, 4096], P(('dp', 'expert')), may hold values from -6 to 6
- select: int32 [4, 128], P(None, ('dp', 'expert')), may hold values from -1 to 127, as said below
- gates: float32 [4, 128], P(None, ('dp', 'expert')), may hold values from 0.1 to 1
- w_gate: bfloat16 [4, 4096, 8192], P('expert', None, 'dp'), may hold values from -0.09375 to 0.09375
- w_up: bfloat16 [4, 4096, 8192], P('expert', None, 'dp'), may hold values from -0.09375 to 0.09375
- w_down: bfloat16 [4, 8192, 4096], P('expert', 'dp'), may hold values from -0.0625 to 0.0625
Outputs:
- mixed: bfloat16 [4096, 4096], P(('dp', 'expert'))
Inputs may be any that keep to these rules, and one draw needn't show every extreme that they name: `select`: in each block of 4 slots of a row, the live entries come first, distinct and ascending, below 128, followed by -1; every block holds at least one live entry, and every expert fills all 4 slots of some source device.
All inputs are finite; a program needn't handle non-finite values.
Results may differ from a plain program's by a relative error of at most 0.0085.
Values may be sent and summed in bfloat16 or wider, within the bound.
A program may use at most 64 MiB of HBM per device.

v0:
```python
import functools

import jax
import jax.numpy as jnp
from jax import lax
from jax.experimental import pallas as pl
from jax.experimental.pallas import tpu as pltpu
from jax.sharding import PartitionSpec as P

MESH = pl.DeviceIdType.MESH
TILE = 16
F32 = jnp.float32
BF16 = jnp.bfloat16


def log2(n):
    return n.bit_length() - 1


def kernel(
    nd, ne, tok, sel, gat, wg_hbm, wu_hbm, wd_hbm, out,
    wg, wu, wd, sb, ab, x, g_acc, u_acc, hid, pb, xr, zb, zr, summed, rb, ob, cmb,
    w_sem, a_send, a_recv, gz_send, gz_recv, gx_send, gx_recv,
    rx_send, rx_recv, rz_send, rz_recv, o_send, o_recv,
):
    stages = x.shape[0]
    inner = x.shape[1]
    outer = x.shape[2]
    rows = x.shape[3]
    span = x.shape[4]
    slots = sel.shape[1]
    tokens_here = tok.shape[0]
    parts = TILE // slots
    wide = span // parts
    chunks = pb.shape[0]
    cols = pb.shape[4]
    dp = lax.axis_index("dp")
    ex = lax.axis_index("expert")
    za = dp // inner
    xb = lax.rem(dp, inner)
    other = (inner - 1) - xb

    def at_expert(d):
        return (dp, lax.rem(ex + d, ne))

    def at_outer(d):
        return (lax.rem(za + d, outer) * inner + xb, ex)

    partner = (za * inner + other, ex)

    def remote(src, dst, send, recv, to):
        return pltpu.make_async_remote_copy(
            src_ref=src, dst_ref=dst, send_sem=send, recv_sem=recv,
            device_id=to, device_id_type=MESH,
        )

    barrier = pltpu.get_barrier_semaphore()
    for d in range(1, ne):
        pl.semaphore_signal(barrier, inc=1, device_id=at_expert(d), device_id_type=MESH)
    for d in range(1, outer):
        pl.semaphore_signal(barrier, inc=1, device_id=at_outer(d), device_id_type=MESH)
    if inner > 1:
        pl.semaphore_signal(barrier, inc=1, device_id=partner, device_id_type=MESH)

    loads = [
        pltpu.make_async_copy(h.at[0], v, w_sem.at[i])
        for i, (h, v) in enumerate(((wg_hbm, wg), (wu_hbm, wu), (wd_hbm, wd)))
    ]
    for load in loads:
        load.start()

    packed = ne * TILE
    r_id = lax.broadcasted_iota(jnp.int32, (packed, tokens_here), 0)
    t_id = lax.broadcasted_iota(jnp.int32, (packed, tokens_here), 1)
    r_slot = ((r_id >> log2(TILE)) << log2(slots)) + (r_id & (slots - 1))
    r_part = (r_id & (TILE - 1)) >> log2(slots)
    named = jnp.full((packed, tokens_here), -1, jnp.int32)
    for e in range(ne):
        for s in range(slots):
            named = jnp.where(r_slot == e * slots + s, sel[e, s], named)
    hit = jnp.where(named == t_id, 1.0, 0.0)
    pick = jnp.concatenate(
        [jnp.where(r_part == p, hit, 0.0).astype(BF16) for p in range(parts)], axis=1
    )
    for q in range(stages):
        stack = jnp.concatenate(
            [tok[:, q * span + p * wide:q * span + (p + 1) * wide] for p in range(parts)], axis=0
        )
        gathered = jnp.dot(pick, stack, preferred_element_type=F32).astype(BF16)
        sb[q] = gathered.reshape(ne, TILE, wide)
        ab[q, ex] = sb[q, ex]

    pl.semaphore_wait(barrier, (ne - 1) + (outer - 1) + (1 if inner > 1 else 0))

    sent = []

    def start(copy):
        copy.start()
        sent.append(copy)

    for q in range(stages):
        for d in range(1, ne):
            to = at_expert(d)
            start(remote(sb.at[q, to[1]], ab.at[q, ex], a_send.at[q, d], a_recv.at[q, d], to))

    def packing(shape, packed_dim):
        r = lax.broadcasted_iota(jnp.int32, shape, packed_dim)
        k = lax.broadcasted_iota(jnp.int32, shape, 1 - packed_dim)
        col = (
            ((r & (TILE - 1)) >> log2(slots)) * rows
            + ((r >> log2(TILE)) << log2(slots)) + (r & (slots - 1))
        )
        return jnp.where(k == col, 1.0, 0.0).astype(BF16)

    pack = packing((packed, parts * rows), 0)
    unpack = packing((parts * rows, packed), 1)

    def gx(q, owner_b, d):
        block = x.at[q, owner_b, lax.rem(za + outer - d, outer)]
        return remote(block, block, gx_send.at[q, d], gx_recv.at[q, d], partner)

    def gz(q, d, owner_a):
        block = x.at[q, xb, owner_a]
        return remote(block, block, gz_send.at[q, d], gz_recv.at[q, d], at_outer(d))

    order = sorted(range(1, outer), key=lambda d: (min(d, outer - d), d))
    for q in range(stages):
        for d in range(1, ne):
            src = lax.rem(ex + ne - d, ne)
            remote(
                sb.at[q, src], ab.at[q, src], a_send.at[q, d], a_recv.at[q, d], at_expert(d)
            ).wait_recv()
        mine = jnp.dot(
            unpack, ab[q].reshape(packed, wide), preferred_element_type=F32
        ).astype(BF16)
        for p in range(parts):
            x[q, xb, za, :, p * wide:(p + 1) * wide] = mine[p * rows:(p + 1) * rows]
        for d in order:
            start(gz(q, d, za))
        if inner > 1:
            start(gx(q, xb, 0))

    terms = 3
    c_id = lax.broadcasted_iota(jnp.int32, (tokens_here, terms * packed), 1)
    n_id = lax.broadcasted_iota(jnp.int32, (tokens_here, terms * packed), 0)
    c_row = c_id & (packed - 1)
    c_slot = ((c_row >> log2(TILE)) << log2(slots)) + (c_row & (slots - 1))
    weight = jnp.zeros((tokens_here, terms * packed), F32)
    for e in range(ne):
        for s in range(slots):
            weight = jnp.where((c_slot == e * slots + s) & (n_id == sel[e, s]), gat[e, s], weight)
    left = weight
    coef = jnp.zeros_like(weight)
    for i in range(terms):
        term = left.astype(BF16).astype(F32)
        coef = jnp.where((c_id >> log2(packed)) == i, term, coef)
        left = left - term
    c_part = (c_row & (TILE - 1)) >> log2(slots)
    for p in range(parts):
        cmb[p] = jnp.where(c_part == p, coef, 0.0).astype(BF16)

    total_rows = inner * outer * rows
    step = min(256, hid.shape[1])

    def arrive(q):
        for d in order:
            gz(q, d, lax.rem(za + outer - d, outer)).wait_recv()
            if inner > 1:
                start(gx(q, xb, d))

    def multiply(q):
        if inner > 1:
            for d in [0] + order:
                gx(q, other, d).wait_recv()
        if q == 0:
            loads[0].wait()
            loads[1].wait()

        @pl.loop(0, hid.shape[1] // step)
        def _(i):
            at = pl.ds(pl.multiple_of(i * step, step), step)
            block = x[q].reshape(total_rows, span)
            g = jnp.dot(block, wg[q * span:(q + 1) * span, at], preferred_element_type=F32)
            u = jnp.dot(block, wu[q * span:(q + 1) * span, at], preferred_element_type=F32)
            if q > 0:
                g = g + g_acc[:, at]
                u = u + u_acc[:, at]
            if q < stages - 1:
                g_acc[:, at] = g
                u_acc[:, at] = u
            else:
                hid[:, at] = (g / (1.0 + jnp.exp(-g)) * u).astype(BF16)

    for q in range(stages):
        arrive(q)
        if q > 0:
            multiply(q - 1)
    multiply(stages - 1)

    loads[2].wait()

    def rx(c):
        return remote(pb.at[c, other], xr.at[c], rx_send.at[c], rx_recv.at[c], partner)

    @pl.loop(0, chunks)
    def _(c):
        at = pl.ds(pl.multiple_of(c * cols, cols), cols)
        part = jnp.dot(hid[...], wd[:, at], preferred_element_type=F32)
        pb[c] = part.astype(BF16).reshape(inner, outer, rows, cols)
        if inner > 1:
            rx(c).start()

    def rz(c, d):
        to = lax.rem(za + d, outer)
        return remote(zb.at[c, to], zr.at[c, d - 1], rz_send.at[c, d], rz_recv.at[c, d], at_outer(d))

    def inner_sum(c):
        value = pb[c, xb].astype(F32)
        if inner > 1:
            rx(c).wait_recv()
            value = value + xr[c].astype(F32)
        zb[c] = value.astype(BF16)
        for d in order:
            rz(c, d).start()

    per = span // cols

    def outer_sum(c):
        value = zb[c, za].astype(F32)
        for d in order:
            rz(c, d).wait_recv()
            value = value + zr[c, d - 1].astype(F32)
        for k in range(cols // wide):
            p = (c % per) * (cols // wide) + k
            summed[c // per, p] = value[:, k * wide:(k + 1) * wide].astype(BF16)

    def give(q):
        back = jnp.dot(pack, summed[q].reshape(parts * rows, wide), preferred_element_type=F32)
        rb[q] = back.astype(BF16).reshape(ne, TILE, wide)
        ob[q, ex] = rb[q, ex]
        for d in range(1, ne):
            to = at_expert(d)
            start(remote(rb.at[q, to[1]], ob.at[q, ex], o_send.at[q, d], o_recv.at[q, d], to))

    def mix(q):
        for d in range(1, ne):
            src = lax.rem(ex + ne - d, ne)
            remote(
                rb.at[q, src], ob.at[q, src], o_send.at[q, d], o_recv.at[q, d], at_expert(d)
            ).wait_recv()
        got = ob[q].reshape(packed, wide)
        total = jnp.dot(
            cmb[...].reshape(parts * tokens_here, terms * packed),
            jnp.concatenate([got] * terms, axis=0),
            preferred_element_type=F32,
        ).astype(BF16)
        for p in range(parts):
            at = q * span + p * wide
            out[:, at:at + wide] = total[p * tokens_here:(p + 1) * tokens_here]

    lag = min(3, chunks)
    for c in range(chunks + lag):
        if c < chunks:
            inner_sum(c)
        done = c - lag
        if done >= 0:
            outer_sum(done)
            if done % per == per - 1:
                give(done // per)
                if done // per > 0:
                    mix(done // per - 1)
    mix(stages - 1)

    for copy in sent:
        copy.wait_send()

    @pl.loop(0, chunks)
    def _(c):
        if inner > 1:
            rx(c).wait_send()
        for d in range(1, outer):
            rz(c, d).wait_send()


def per_device(nd, ne, tokens, select, gates, w_gate, w_up, w_down):
    tok_dev, width = tokens.shape
    slots = select.shape[1]
    hidden = w_gate.shape[2]
    inner = 2 if nd % 2 == 0 else 1
    outer = nd // inner
    rows = ne * slots
    parts = TILE // slots
    stages = 4
    span = width // stages
    wide = span // parts
    cols = span // 2
    chunks = width // cols
    vmem = pl.BlockSpec(memory_space=pltpu.VMEM)
    smem = pl.BlockSpec(memory_space=pltpu.SMEM)
    hbm = pl.BlockSpec(memory_space=pl.ANY)
    dma = pltpu.SemaphoreType.DMA
    return pl.pallas_call(
        functools.partial(kernel, nd, ne),
        out_shape=jax.ShapeDtypeStruct((tok_dev, width), BF16),
        in_specs=[vmem, smem, smem, hbm, hbm, hbm],
        out_specs=vmem,
        scratch_shapes=[
            pltpu.VMEM((width, hidden), BF16),
            pltpu.VMEM((width, hidden), BF16),
            pltpu.VMEM((hidden, width), BF16),
            pltpu.VMEM((stages, ne, TILE, wide), BF16),
            pltpu.VMEM((stages, ne, TILE, wide), BF16),
            pltpu.VMEM((stages, inner, outer, rows, span), BF16),
            pltpu.VMEM((nd * rows, hidden), F32),
            pltpu.VMEM((nd * rows, hidden), F32),
            pltpu.VMEM((nd * rows, hidden), BF16),
            pltpu.VMEM((chunks, inner, outer, rows, cols), BF16),
            pltpu.VMEM((chunks, outer, rows, cols), BF16),
            pltpu.VMEM((chunks, outer, rows, cols), BF16),
            pltpu.VMEM((chunks, max(outer - 1, 1), rows, cols), BF16),
            pltpu.VMEM((stages, parts, rows, wide), BF16),
            pltpu.VMEM((stages, ne, TILE, wide), BF16),
            pltpu.VMEM((stages, ne, TILE, wide), BF16),
            pltpu.VMEM((parts, tok_dev, 3 * ne * TILE), BF16),
            dma((3,)),
            dma((stages, ne)), dma((stages, ne)),
            dma((stages, outer)), dma((stages, outer)),
            dma((stages, outer)), dma((stages, outer)),
            dma((chunks,)), dma((chunks,)),
            dma((chunks, outer)), dma((chunks, outer)),
            dma((stages, ne)), dma((stages, ne)),
        ],
        compiler_params=pltpu.CompilerParams(
            collective_id=0, has_side_effects=True, vmem_limit_bytes=60 * 1024 * 1024
        ),
    )(tokens, select, gates, w_gate, w_up, w_down)


def solution(mesh):
    return jax.shard_map(
        functools.partial(per_device, mesh.shape["dp"], mesh.shape["expert"]),
        mesh=mesh,
        in_specs=(
            P(("dp", "expert"), None),
            P(None, ("dp", "expert")),
            P(None, ("dp", "expert")),
            P("expert", None, "dp"),
            P("expert", None, "dp"),
            P("expert", "dp", None),
        ),
        out_specs=P(("dp", "expert"), None),
        check_vma=False,
    )
```

profile of v0, /device:TPU:0, one launch (start us, length us, event | category | flops | bytes accessed | tf_op | source)
XLA Modules:
  0.0 54.8 jit_solution(7306230156656343088)
XLA Ops:
  0.0 52.5 %shard_map.64 = bf16[128,4096]{1,0:T(8,128)(2,1)} custom-call(bf16[128,4096]{1,0:T(8,128)(2,1)} %tok.1, s32[4,4]{1,0:T(4,128)} %sel.1, f32[4,4]{1,0:T(4,128)} %gat.1, bf16[1,4096,1024]{2,1,0:T(8,128)(2,1)} %wg_hbm.1, bf16[1,4096,1024]{2,1,0:T(8,128)(2,1)} %wu_hbm.1, bf16[1,1024,4096]{2,1,0:T(8,128)(2,1)} %wd_hbm.1), custom_call_target="tpu_custom_call" | custom-call | tf_op jit(solution)/shard_map/pallas_call | solution.py:302
  52.5 2.3 %copy.8 = bf16[128,4096]{1,0:T(8,128)(2,1)} copy(bf16[128,4096]{1,0:T(8,128)(2,1)} %shard_map.64) | data formatting | bytes 2097152
where the time goes:
time: 54.9 us; the launch traced here: 54.8 us
  Pallas kernels  52.5 us (96%)
  local copies, waits for them, and re-layouts  2.29 us (4%)
    pallas_call x1, Pallas kernels, per_device(): pl.pallas_call(functools.partial(kernel, nd, ne), out_shape=jax.ShapeDtyp...  52.5 us
    unnamed x1, local copies, waits for them, and re-layouts  2.29 us

commit v1 on v0

--- a/solution.py
+++ b/solution.py
@@ -18,9 +18,9 @@
 
 
 def kernel(
-    nd, ne, tok, sel, gat, wg_hbm, wu_hbm, wd_hbm, out,
-    wg, wu, wd, sb, ab, x, g_acc, u_acc, hid, pb, xr, zb, zr, summed, rb, ob, cmb,
-    w_sem, a_send, a_recv, gz_send, gz_recv, gx_send, gx_recv,
+    nd, ne, tok_hbm, sel, gat, wg_hbm, wu_hbm, wd_hbm, ob, cmb,
+    tok, wg, wu, wd, sb, ab, x, g_acc, u_acc, hid, pb, xr, zb, zr, summed, rb,
+    t_sem, w_sem, a_send, a_recv, gz_send, gz_recv, gx_send, gx_recv,
     rx_send, rx_recv, rz_send, rz_recv, o_send, o_recv,
 ):
     stages = x.shape[0]
@@ -62,6 +62,8 @@
     if inner > 1:
         pl.semaphore_signal(barrier, inc=1, device_id=partner, device_id_type=MESH)
 
+    fetch = pltpu.make_async_copy(tok_hbm, tok, t_sem)
+    fetch.start()
     loads = [
         pltpu.make_async_copy(h.at[0], v, w_sem.at[i])
         for i, (h, v) in enumerate(((wg_hbm, wg), (wu_hbm, wu), (wd_hbm, wd)))
@@ -82,6 +84,7 @@
     pick = jnp.concatenate(
         [jnp.where(r_part == p, hit, 0.0).astype(BF16) for p in range(parts)], axis=1
     )
+    fetch.wait()
     for q in range(stages):
         stack = jnp.concatenate(
             [tok[:, q * span + p * wide:q * span + (p + 1) * wide] for p in range(parts)], axis=0
@@ -176,7 +179,7 @@
             loads[0].wait()
             loads[1].wait()
 
-        @pl.loop(0, hid.shape[1] // step)
+        @pl.loop(0, hid.shape[1] // step, unroll=True)
         def _(i):
             at = pl.ds(pl.multiple_of(i * step, step), step)
             block = x[q].reshape(total_rows, span)
@@ -242,22 +245,6 @@
             to = at_expert(d)
             start(remote(rb.at[q, to[1]], ob.at[q, ex], o_send.at[q, d], o_recv.at[q, d], to))
 
-    def mix(q):
-        for d in range(1, ne):
-            src = lax.rem(ex + ne - d, ne)
-            remote(
-                rb.at[q, src], ob.at[q, src], o_send.at[q, d], o_recv.at[q, d], at_expert(d)
-            ).wait_recv()
-        got = ob[q].reshape(packed, wide)
-        total = jnp.dot(
-            cmb[...].reshape(parts * tokens_here, terms * packed),
-            jnp.concatenate([got] * terms, axis=0),
-            preferred_element_type=F32,
-        ).astype(BF16)
-        for p in range(parts):
-            at = q * span + p * wide
-            out[:, at:at + wide] = total[p * tokens_here:(p + 1) * tokens_here]
-
     lag = min(3, chunks)
     for c in range(chunks + lag):
         if c < chunks:
@@ -267,9 +254,13 @@
             outer_sum(done)
             if done % per == per - 1:
                 give(done // per)
-                if done // per > 0:
-                    mix(done // per - 1)
-    mix(stages - 1)
+
+    for q in range(stages):
+        for d in range(1, ne):
+            src = lax.rem(ex + ne - d, ne)
+            remote(
+                rb.at[q, src], ob.at[q, src], o_send.at[q, d], o_recv.at[q, d], at_expert(d)
+            ).wait_recv()
 
     for copy in sent:
         copy.wait_send()
@@ -280,6 +271,31 @@
             rx(c).wait_send()
         for d in range(1, outer):
             rz(c, d).wait_send()
+
+
+def mix(ob, cmb, out_hbm, out, sem):
+    stages, ne, tile, wide = ob.shape
+    parts, tokens_here, depth = cmb.shape
+    packed = ne * tile
+    terms = depth // packed
+    span = parts * wide
+    stores = []
+    for q in range(stages):
+        got = ob[q].reshape(packed, wide)
+        total = jnp.dot(
+            cmb[...].reshape(parts * tokens_here, depth),
+            jnp.concatenate([got] * terms, axis=0),
+            preferred_element_type=F32,
+        ).astype(BF16)
+        for p in range(parts):
+            at = q * span + p * wide
+            out[:, at:at + wide] = total[p * tokens_here:(p + 1) * tokens_here]
+        at = pl.ds(q * span, span)
+        store = pltpu.make_async_copy(out.at[:, at], out_hbm.at[:, at], sem.at[q])
+        store.start()
+        stores.append(store)
+    for store in stores:
+        store.wait()
 
 
 def per_device(nd, ne, tokens, select, gates, w_gate, w_up, w_down):
@@ -299,12 +315,16 @@
     smem = pl.BlockSpec(memory_space=pltpu.SMEM)
     hbm = pl.BlockSpec(memory_space=pl.ANY)
     dma = pltpu.SemaphoreType.DMA
-    return pl.pallas_call(
+    returned, coef = pl.pallas_call(
         functools.partial(kernel, nd, ne),
-        out_shape=jax.ShapeDtypeStruct((tok_dev, width), BF16),
-        in_specs=[vmem, smem, smem, hbm, hbm, hbm],
-        out_specs=vmem,
+        out_shape=(
+            jax.ShapeDtypeStruct((stages, ne, TILE, wide), BF16),
+            jax.ShapeDtypeStruct((parts, tok_dev, 3 * ne * TILE), BF16),
+        ),
+        in_specs=[hbm, smem, smem, hbm, hbm, hbm],
+        out_specs=(vmem, vmem),
         scratch_shapes=[
+            pltpu.VMEM((tok_dev, width), BF16),
             pltpu.VMEM((width, hidden), BF16),
             pltpu.VMEM((width, hidden), BF16),
             pltpu.VMEM((hidden, width), BF16),
@@ -320,8 +340,7 @@
             pltpu.VMEM((chunks, max(outer - 1, 1), rows, cols), BF16),
             pltpu.VMEM((stages, parts, rows, wide), BF16),
             pltpu.VMEM((stages, ne, TILE, wide), BF16),
-            pltpu.VMEM((stages, ne, TILE, wide), BF16),
-            pltpu.VMEM((parts, tok_dev, 3 * ne * TILE), BF16),
+            dma(()),
             dma((3,)),
             dma((stages, ne)), dma((stages, ne)),
             dma((stages, outer)), dma((stages, outer)),
@@ -334,6 +353,13 @@
             collective_id=0, has_side_effects=True, vmem_limit_bytes=60 * 1024 * 1024
         ),
     )(tokens, select, gates, w_gate, w_up, w_down)
+    return pl.pallas_call(
+        mix,
+        out_shape=jax.ShapeDtypeStruct((tok_dev, width), BF16),
+        in_specs=[vmem, vmem],
+        out_specs=hbm,
+        scratch_shapes=[pltpu.VMEM((tok_dev, width), BF16), dma((stages,))],
+    )(returned, coef)
 
 
 def solution(mesh):

time: 54.9 us -> 55.1 us (level)
  Pallas kernels: 52.5 us -> 55 us
  local copies, waits for them, and re-layouts: 2.29 us -> 0 us
    pallas_call x1 -> x2, Pallas kernels: 52.5 us -> 55 us  [the longest x1 52.6 us: per_device(): pl.pallas_call(functools.partial(kernel, nd, ne), out_shape=(jax.ShapeDty...]
    unnamed x1 -> x0, local copies, waits for them, and re-layouts: 2.29 us -> none
where the time goes in v1:
time: 55.1 us; the launch traced here: 55 us
  Pallas kernels  55 us (100%)
    pallas_call x1, Pallas kernels, per_device(): pl.pallas_call(functools.partial(kernel, nd, ne), out_shape=(jax.ShapeDty...  52.6 us
    pallas_call x1, Pallas kernels, per_device(): pl.pallas_call(mix, out_shape=jax.ShapeDtypeStruct((tok_dev, width), BF16...  2.31 us

profile of v1, /device:TPU:0, one launch (start us, length us, event | category | flops | bytes accessed | tf_op | source)
XLA Modules:
  0.0 55.0 jit_solution(730372056332964511)
XLA Ops:
  0.0 52.6 %shard_map.64 = (bf16[4,4,16,256]{3,2,1,0:T(8,128)(2,1)}, bf16[4,128,192]{2,1,0:T(8,128)(2,1)}) custom-call(bf16[128,4096]{1,0:T(8,128)(2,1)} %tok_hbm.1, s32[4,4]{1,0:T(4,128)} %sel.1, f32[4,4]{1,0:T(4,128)} %gat.1, bf16[1,4096,1024]{2,1,0:T(8,128)(2,1)} %wg_hbm.1, bf16[1,4096,1024]{2,1,0:T(8,128)(2,1)} %wu_hbm.1, bf16[1,1024,4096]{2,1,0:T(8,128)(2,1)} %wd_hbm.1), custom_call_target="tpu_custom_call" | custom-call | tf_op jit(solution)/shard_map/pallas_call | solution.py:318
  52.7 2.3 %shard_map.65 = bf16[128,4096]{1,0:T(8,128)(2,1)} custom-call(bf16[4,4,16,256]{3,2,1,0:T(8,128)(2,1)} %get-tuple-element.7.ob, bf16[4,128,192]{2,1,0:T(8,128)(2,1)} %get-tuple-element.8.cmb), custom_call_target="tpu_custom_call" | custom-call | tf_op jit(solution)/shard_map/pallas_call | solution.py:356

commit v2 on v1

--- a/solution.py
+++ b/solution.py
@@ -18,9 +18,9 @@
 
 
 def kernel(
-    nd, ne, tok_hbm, sel, gat, wg_hbm, wu_hbm, wd_hbm, ob, cmb,
-    tok, wg, wu, wd, sb, ab, x, g_acc, u_acc, hid, pb, xr, zb, zr, summed, rb,
-    t_sem, w_sem, a_send, a_recv, gz_send, gz_recv, gx_send, gx_recv,
+    nd, ne, tok_hbm, sel_hbm, gat_hbm, wg_hbm, wu_hbm, wd_hbm, ob, cmb,
+    tok, sel, gat, wg, wu, wd, sb, ab, x, g_acc, u_acc, hid, pb, xr, zb, zr, summed, rb,
+    t_sem, s_sem, w_sem, a_send, a_recv, gz_send, gz_recv, gx_send, gx_recv,
     rx_send, rx_recv, rz_send, rz_recv, o_send, o_recv,
 ):
     stages = x.shape[0]
@@ -54,6 +54,14 @@
             device_id=to, device_id_type=MESH,
         )
 
+    fetch = pltpu.make_async_copy(tok_hbm, tok, t_sem)
+    fetch.start()
+    small = [
+        pltpu.make_async_copy(h, v, s_sem.at[i])
+        for i, (h, v) in enumerate(((sel_hbm, sel), (gat_hbm, gat)))
+    ]
+    for copy in small:
+        copy.start()
     barrier = pltpu.get_barrier_semaphore()
     for d in range(1, ne):
         pl.semaphore_signal(barrier, inc=1, device_id=at_expert(d), device_id_type=MESH)
@@ -62,16 +70,8 @@
     if inner > 1:
         pl.semaphore_signal(barrier, inc=1, device_id=partner, device_id_type=MESH)
 
-    fetch = pltpu.make_async_copy(tok_hbm, tok, t_sem)
-    fetch.start()
-    loads = [
-        pltpu.make_async_copy(h.at[0], v, w_sem.at[i])
-        for i, (h, v) in enumerate(((wg_hbm, wg), (wu_hbm, wu), (wd_hbm, wd)))
-    ]
-    for load in loads:
-        load.start()
-
     packed = ne * TILE
+    small[0].wait()
     r_id = lax.broadcasted_iota(jnp.int32, (packed, tokens_here), 0)
     t_id = lax.broadcasted_iota(jnp.int32, (packed, tokens_here), 1)
     r_slot = ((r_id >> log2(TILE)) << log2(slots)) + (r_id & (slots - 1))
@@ -85,6 +85,13 @@
         [jnp.where(r_part == p, hit, 0.0).astype(BF16) for p in range(parts)], axis=1
     )
     fetch.wait()
+    loads = [
+        pltpu.make_async_copy(h.at[0], v, w_sem.at[i])
+        for i, (h, v) in enumerate(((wg_hbm, wg), (wu_hbm, wu), (wd_hbm, wd)))
+    ]
+    for load in loads:
+        load.start()
+
     for q in range(stages):
         stack = jnp.concatenate(
             [tok[:, q * span + p * wide:q * span + (p + 1) * wide] for p in range(parts)], axis=0
@@ -95,16 +102,13 @@
 
     pl.semaphore_wait(barrier, (ne - 1) + (outer - 1) + (1 if inner > 1 else 0))
 
-    sent = []
-
     def start(copy):
         copy.start()
-        sent.append(copy)
 
     for q in range(stages):
         for d in range(1, ne):
             to = at_expert(d)
-            start(remote(sb.at[q, to[1]], ab.at[q, ex], a_send.at[q, d], a_recv.at[q, d], to))
+            start(remote(sb.at[q, to[1]], ab.at[q, ex], a_send, a_recv.at[q, d], to))
 
     def packing(shape, packed_dim):
         r = lax.broadcasted_iota(jnp.int32, shape, packed_dim)
@@ -120,18 +124,18 @@
 
     def gx(q, owner_b, d):
         block = x.at[q, owner_b, lax.rem(za + outer - d, outer)]
-        return remote(block, block, gx_send.at[q, d], gx_recv.at[q, d], partner)
+        return remote(block, block, gx_send, gx_recv.at[q, d], partner)
 
     def gz(q, d, owner_a):
         block = x.at[q, xb, owner_a]
-        return remote(block, block, gz_send.at[q, d], gz_recv.at[q, d], at_outer(d))
+        return remote(block, block, gz_send, gz_recv.at[q, d], at_outer(d))
 
     order = sorted(range(1, outer), key=lambda d: (min(d, outer - d), d))
     for q in range(stages):
         for d in range(1, ne):
             src = lax.rem(ex + ne - d, ne)
             remote(
-                sb.at[q, src], ab.at[q, src], a_send.at[q, d], a_recv.at[q, d], at_expert(d)
+                sb.at[q, src], ab.at[q, src], a_send, a_recv.at[q, d], at_expert(d)
             ).wait_recv()
         mine = jnp.dot(
             unpack, ab[q].reshape(packed, wide), preferred_element_type=F32
@@ -148,6 +152,7 @@
     n_id = lax.broadcasted_iota(jnp.int32, (tokens_here, terms * packed), 0)
     c_row = c_id & (packed - 1)
     c_slot = ((c_row >> log2(TILE)) << log2(slots)) + (c_row & (slots - 1))
+    small[1].wait()
     weight = jnp.zeros((tokens_here, terms * packed), F32)
     for e in range(ne):
         for s in range(slots):
@@ -203,7 +208,7 @@
     loads[2].wait()
 
     def rx(c):
-        return remote(pb.at[c, other], xr.at[c], rx_send.at[c], rx_recv.at[c], partner)
+        return remote(pb.at[c, other], xr.at[c], rx_send, rx_recv.at[c], partner)
 
     @pl.loop(0, chunks)
     def _(c):
@@ -215,7 +220,7 @@
 
     def rz(c, d):
         to = lax.rem(za + d, outer)
-        return remote(zb.at[c, to], zr.at[c, d - 1], rz_send.at[c, d], rz_recv.at[c, d], at_outer(d))
+        return remote(zb.at[c, to], zr.at[c, d - 1], rz_send, rz_recv.at[c, d], at_outer(d))
 
     def inner_sum(c):
         value = pb[c, xb].astype(F32)
@@ -243,7 +248,7 @@
         ob[q, ex] = rb[q, ex]
         for d in range(1, ne):
             to = at_expert(d)
-            start(remote(rb.at[q, to[1]], ob.at[q, ex], o_send.at[q, d], o_recv.at[q, d], to))
+            start(remote(rb.at[q, to[1]], ob.at[q, ex], o_send, o_recv.at[q, d], to))
 
     lag = min(3, chunks)
     for c in range(chunks + lag):
@@ -259,18 +264,20 @@
         for d in range(1, ne):
             src = lax.rem(ex + ne - d, ne)
             remote(
-                rb.at[q, src], ob.at[q, src], o_send.at[q, d], o_recv.at[q, d], at_expert(d)
+                rb.at[q, src], ob.at[q, src], o_send, o_recv.at[q, d], at_expert(d)
             ).wait_recv()
 
-    for copy in sent:
-        copy.wait_send()
-
-    @pl.loop(0, chunks)
-    def _(c):
-        if inner > 1:
-            rx(c).wait_send()
-        for d in range(1, outer):
-            rz(c, d).wait_send()
+    def drain(block, sem, to):
+        remote(block, block, sem, sem, to).wait_send()
+
+    drain(sb.at[:, 0:ne - 1], a_send, at_expert(1))
+    drain(rb.at[:, 0:ne - 1], o_send, at_expert(1))
+    if outer > 1:
+        drain(x.at[:, 0, 0:outer - 1], gz_send, at_outer(1))
+        drain(zb.at[:, 0:outer - 1], rz_send, at_outer(1))
+    if inner > 1:
+        drain(x.at[:, 0], gx_send, partner)
+        drain(pb.at[:, 0], rx_send, partner)
 
 
 def mix(ob, cmb, out_hbm, out, sem):
@@ -312,19 +319,20 @@
     cols = span // 2
     chunks = width // cols
     vmem = pl.BlockSpec(memory_space=pltpu.VMEM)
-    smem = pl.BlockSpec(memory_space=pltpu.SMEM)
     hbm = pl.BlockSpec(memory_space=pl.ANY)
     dma = pltpu.SemaphoreType.DMA
     returned, coef = pl.pallas_call(
         functools.partial(kernel, nd, ne),
         out_shape=(
-            jax.ShapeDtypeStruct((stages, ne, TILE, wide), BF16),
-            jax.ShapeDtypeStruct((parts, tok_dev, 3 * ne * TILE), BF16),
+            pltpu.VMEM((stages, ne, TILE, wide), BF16),
+            pltpu.VMEM((parts, tok_dev, 3 * ne * TILE), BF16),
         ),
-        in_specs=[hbm, smem, smem, hbm, hbm, hbm],
+        in_specs=[hbm] * 6,
         out_specs=(vmem, vmem),
         scratch_shapes=[
             pltpu.VMEM((tok_dev, width), BF16),
+            pltpu.SMEM(select.shape, jnp.int32),
+            pltpu.SMEM(gates.shape, F32),
             pltpu.VMEM((width, hidden), BF16),
             pltpu.VMEM((width, hidden), BF16),
             pltpu.VMEM((hidden, width), BF16),
@@ -340,14 +348,14 @@
             pltpu.VMEM((chunks, max(outer - 1, 1), rows, cols), BF16),
             pltpu.VMEM((stages, parts, rows, wide), BF16),
             pltpu.VMEM((stages, ne, TILE, wide), BF16),
-            dma(()),
+            dma(()), dma((2,)),
             dma((3,)),
-            dma((stages, ne)), dma((stages, ne)),
-            dma((stages, outer)), dma((stages, outer)),
-            dma((stages, outer)), dma((stages, outer)),
-            dma((chunks,)), dma((chunks,)),
-            dma((chunks, outer)), dma((chunks, outer)),
-            dma((stages, ne)), dma((stages, ne)),
+            dma(()), dma((stages, ne)),
+            dma(()), dma((stages, outer)),
+            dma(()), dma((stages, outer)),
+            dma(()), dma((chunks,)),
+            dma(()), dma((chunks, outer)),
+            dma(()), dma((stages, ne)),
         ],
         compiler_params=pltpu.CompilerParams(
             collective_id=0, has_side_effects=True, vmem_limit_bytes=60 * 1024 * 1024
@@ -359,7 +367,7 @@
         in_specs=[vmem, vmem],
         out_specs=hbm,
         scratch_shapes=[pltpu.VMEM((tok_dev, width), BF16), dma((stages,))],
-    )(returned, coef)
+    )(pltpu.with_memory_space_constraint(returned, pltpu.VMEM), pltpu.with_memory_space_constraint(coef, pltpu.VMEM))
 
 
 def solution(mesh):

time: 55.1 us -> 47 us (0.85)
  Pallas kernels: 55 us -> 46.8 us
    pallas_call x1, Pallas kernels: 52.6 us -> 45.5 us  [per_device(): pl.pallas_call(functools.partial(kernel, nd, ne), out_shape=(pltpu.VMEM((...]
    pallas_call x1, Pallas kernels: 2.31 us -> 1.29 us  [per_device(): pl.pallas_call(mix, out_shape=jax.ShapeDtypeStruct((tok_dev, width), BF16...]
where the time goes in v2:
time: 47 us; the launch traced here: 46.8 us
  Pallas kernels  46.8 us (100%)
    pallas_call x1, Pallas kernels, per_device(): pl.pallas_call(functools.partial(kernel, nd, ne), out_shape=(pltpu.VMEM((...  45.5 us
    pallas_call x1, Pallas kernels, per_device(): pl.pallas_call(mix, out_shape=jax.ShapeDtypeStruct((tok_dev, width), BF16...  1.29 us

profile of v2, /device:TPU:0, one launch (start us, length us, event | category | flops | bytes accessed | tf_op | source)
XLA Modules:
  0.0 46.8 jit_solution(12960172157398031356)
XLA Ops:
  0.0 45.5 %shard_map.64 = (bf16[4,4,16,256]{3,2,1,0:T(8,128)(2,1)S(1)}, bf16[4,128,192]{2,1,0:T(8,128)(2,1)S(1)}) custom-call(bf16[128,4096]{1,0:T(8,128)(2,1)} %tok_hbm.1, s32[4,4]{1,0:T(4,128)} %sel_hbm.1, f32[4,4]{1,0:T(4,128)} %gat_hbm.1, bf16[1,4096,1024]{2,1,0:T(8,128)(2,1)} %wg_hbm.1, bf16[1,4096,1024]{2,1,0:T(8,128)(2,1)} %wu_hbm.1, bf16[1,1024,4096]{2,1,0:T(8,128)(2,1)} %wd_hbm.1), custom_call_target="tpu_custom_call" | custom-call | tf_op jit(solution)/shard_map/pallas_call | solution.py:324
  45.5 1.3 %shard_map.65 = bf16[128,4096]{1,0:T(8,128)(2,1)} custom-call(bf16[4,4,16,256]{3,2,1,0:T(8,128)(2,1)S(1)} %get-tuple-element.7.ob, bf16[4,128,192]{2,1,0:T(8,128)(2,1)S(1)} %get-tuple-element.8.cmb), custom_call_target="tpu_custom_call" | custom-call | tf_op jit(solution)/shard_map/pallas_call | solution.py:364

commit v3 on v2

v3 whole, which is shorter than its diff:
```python
import functools

import jax
import jax.numpy as jnp
from jax import lax
from jax.experimental import pallas as pl
from jax.experimental.pallas import tpu as pltpu
from jax.sharding import PartitionSpec as P

MESH = pl.DeviceIdType.MESH
TILE = 16
F32 = jnp.float32
BF16 = jnp.bfloat16
scope = jax.named_scope


def log2(n):
    return n.bit_length() - 1


def kernel(
    nd, ne, tok_hbm, sel_hbm, gat_hbm, wg_hbm, wu_hbm, wd_hbm, ob, cmb,
    tok, sel, gat, wg, wu, wd, sb, xp, unp, xs, g_acc, u_acc, hid, pb, xr, zb, zr, summed, rb,
    l_sem, w_sem, a_send, a_recv, gz_send, gf_send, gz_recv, gx_send, gx_recv,
    rx_send, rx_recv, rz_send, rz_recv, o_send, o_recv,
):
    batches, stages, inner, outer, each, _, wide = xp.shape
    slots = sel.shape[1]
    tokens_here = tok.shape[0]
    parts = TILE // slots
    span = wide * parts
    rows = each * slots
    chunks = pb.shape[1]
    tile_rows, tile_cols = pb.shape[4:]
    fold = tile_rows // rows
    cols = fold * tile_cols
    units = ob.shape[0]
    per = chunks // units
    packed = ne * TILE
    total_rows = inner * outer * rows
    half = outer // 2
    pair = 2 if ne % 2 == 0 else 1
    chips = ne // pair
    dp = lax.axis_index("dp")
    ex = lax.axis_index("expert")
    za = dp // inner
    xb = lax.rem(dp, inner)
    other = (inner - 1) - xb
    chip = ex // pair
    core = lax.rem(ex, pair)

    def at_expert(t):
        to_chip = lax.rem(chip + t // pair, chips)
        return to_chip * pair + lax.rem(core + t % pair, pair)

    def at_z(z):
        return (z * inner + xb, ex)

    def at_outer(d):
        return at_z(lax.rem(za + d, outer))

    partner = (za * inner + other, ex)

    def remote(src, dst, send, recv, to):
        return pltpu.make_async_remote_copy(
            src_ref=src, dst_ref=dst, send_sem=send, recv_sem=recv,
            device_id=to, device_id_type=MESH,
        )

    fetch = pltpu.make_async_copy(tok_hbm, tok, l_sem.at[0])
    fetch.start()
    get_sel = pltpu.make_async_copy(sel_hbm, sel, l_sem.at[1])
    get_sel.start()
    get_gat = pltpu.make_async_copy(gat_hbm, gat, l_sem.at[2])
    get_gat.start()
    barrier = pltpu.get_barrier_semaphore()
    for t in range(1, ne):
        pl.semaphore_signal(barrier, inc=1, device_id=(dp, at_expert(t)), device_id_type=MESH)
    for d in range(1, outer):
        pl.semaphore_signal(barrier, inc=1, device_id=at_outer(d), device_id_type=MESH)
    if inner > 1:
        pl.semaphore_signal(barrier, inc=1, device_id=partner, device_id_type=MESH)

    get_sel.wait()
    r_id = lax.broadcasted_iota(jnp.int32, (packed, tokens_here), 0)
    t_id = lax.broadcasted_iota(jnp.int32, (packed, tokens_here), 1)
    r_slot = ((r_id >> log2(TILE)) << log2(slots)) + (r_id & (slots - 1))
    r_part = (r_id & (TILE - 1)) >> log2(slots)
    named = jnp.full((packed, tokens_here), -1, jnp.int32)
    for e in range(ne):
        for s in range(slots):
            named = jnp.where(r_slot == e * slots + s, sel[e, s], named)
    hit = jnp.where(named == t_id, 1.0, 0.0)
    pick = jnp.concatenate(
        [jnp.where(r_part == p, hit, 0.0).astype(BF16) for p in range(parts)], axis=1
    )
    with scope("fetch"):
        fetch.wait()
    loads = [
        pltpu.make_async_copy(h.at[0], v, w_sem.at[i])
        for i, (h, v) in enumerate(((wg_hbm, wg), (wu_hbm, wu), (wd_hbm, wd)))
    ]
    for load in loads:
        load.start()

    def place(e, j):
        r = lax.rem(j - (e // pair) * pair + ne, ne)
        return r // each, lax.rem(r, each)

    mine = place(ex, ex)[1]
    for q in range(stages):
        stack = jnp.concatenate(
            [tok[:, q * span + p * wide:q * span + (p + 1) * wide] for p in range(parts)], axis=0
        )
        gathered = jnp.dot(pick, stack, preferred_element_type=F32).astype(BF16)
        sb[q] = gathered.reshape(ne, TILE, wide)
        xp[0, q, xb, za, mine] = sb[q, ex]

    with scope("barrier"):
        pl.semaphore_wait(barrier, (ne - 1) + (outer - 1) + (1 if inner > 1 else 0))

    for t in range(1, ne):
        for q in range(stages):
            e = at_expert(t)
            b, k = place(e, ex)
            remote(
                sb.at[q, e], xp.at[b, q, xb, za, k], a_send, a_recv.at[b, q], (dp, e)
            ).start()

    relayed = outer >= 4 and outer % 2 == 0
    my_half = za // max(half, 1)
    near_gate = half - 1 + my_half
    far_gate = half - my_half

    def is_relayed(b, q):
        return relayed and RELAY[b]

    def targets(b, q):
        if not is_relayed(b, q):
            return [lax.rem(za + d, outer) for d in sorted(range(1, outer), key=lambda d: min(d, outer - d))]
        mates = [my_half * half + lax.rem(za - my_half * half + i, half) for i in range(1, half)]
        return mates + [far_gate]

    def send_own(b, q, k, n):
        block = xp.at[b, q, xb, za, pl.ds(k, n)]
        if inner > 1:
            remote(block, block, gx_send, gx_recv.at[b, q], partner).start()
        for z in targets(b, q):
            remote(block, block, gz_send.at[b], gz_recv.at[b, q, za], at_z(z)).start()

    def own_first(q):
        send_own(0, q, mine, 1)

    def own(b, q):
        arrived = xp.at[b, q, xb, za, pl.ds(0, each - 1 if b == 0 else each)]
        if b > 0:
            remote(arrived, arrived, a_send, a_recv.at[b, q], partner).wait_recv()
            send_own(b, q, 0, each)
        elif each > 1:
            remote(arrived, arrived, a_send, a_recv.at[b, q], partner).wait_recv()
            for i in range(1, each):
                send_own(b, q, lax.rem(mine + i, each), 1)

    def take(b, q, z):
        block = xp.at[b, q, xb, z]
        remote(block, block, gz_send.at[b], gz_recv.at[b, q, z], partner).wait_recv()
        if inner > 1:
            remote(block, block, gx_send, gx_recv.at[b, q], partner).start()

    def mate(i):
        return my_half * half + lax.rem(za - my_half * half + i, half)

    def arrive(b, q):
        if not is_relayed(b, q):
            for d in sorted(range(1, outer), key=lambda d: min(d, outer - d)):
                take(b, q, lax.rem(za + outer - d, outer))
            return
        for i in range(1, half):
            take(b, q, mate(i))

    def far_side():
        return [far_gate + i * (1 - 2 * my_half) for i in range(half)]

    def relay(b, q):
        if not is_relayed(b, q):
            return

        @pl.when(za == near_gate)
        def _():
            for z in far_side():
                take(b, q, z)
                block = xp.at[b, q, xb, z]
                for i in range(1, half):
                    remote(
                        block, block, gf_send.at[b, i - 1], gz_recv.at[b, q, z], at_z(mate(i))
                    ).start()

    def distant(b, q):
        if not is_relayed(b, q):
            return

        @pl.when(za != near_gate)
        def _():
            for z in far_side():
                take(b, q, z)

    def spread():
        r = lax.broadcasted_iota(jnp.int32, unp.shape, 0)
        k = lax.broadcasted_iota(jnp.int32, unp.shape, 1)
        part = r >> log2(total_rows)
        row = r & (total_rows - 1)
        col = ((row >> log2(slots)) << log2(TILE)) + (part << log2(slots)) + (row & (slots - 1))
        unp[...] = jnp.where(k == col, 1.0, 0.0).astype(BF16)

    step = min(256, hid.shape[1])
    blocks = hid.shape[1] // step

    def ready(b, q):
        if inner > 1:
            block = xp.at[b, q, other]
            remote(block, block, gx_send, gx_recv.at[b, q], partner).wait_recv()
        if b == 0 and q == 0:
            loads[0].wait()
            loads[1].wait()
        flat = jnp.dot(
            unp[...], xp[b, q].reshape(parts * total_rows, wide), preferred_element_type=F32
        ).astype(BF16)
        for p in range(parts):
            xs[:, p * wide:(p + 1) * wide] = flat[p * total_rows:(p + 1) * total_rows]

    def multiply(b, q, i):
        at = pl.ds(i * step, step)
        g = jnp.dot(xs[...], wg[q * span:(q + 1) * span, at], preferred_element_type=F32)
        u = jnp.dot(xs[...], wu[q * span:(q + 1) * span, at], preferred_element_type=F32)
        if q > 0:
            g = g + g_acc[:, at]
            u = u + u_acc[:, at]
        if q < stages - 1:
            g_acc[:, at] = g
            u_acc[:, at] = u
        else:
            hid[:, at] = (g / (1.0 + jnp.exp(-g)) * u).astype(BF16)

    def rx(b, c):
        return remote(pb.at[b, c, other], xr.at[b, c], rx_send, rx_recv.at[b, c], partner)

    def down(b, c):
        if b == 0 and c == 0:
            loads[2].wait()
        at = pl.ds(c * cols, cols)
        part = jnp.dot(hid[...], wd[:, at], preferred_element_type=F32)
        part = part.reshape(inner, outer, rows, cols)
        part = jnp.concatenate(
            [part[..., f * tile_cols:(f + 1) * tile_cols] for f in range(fold)], axis=2
        )
        pb[b, c] = part.astype(BF16)
        if inner > 1:
            rx(b, c).start()

    def inner_sum(b, c):
        value = pb[b, c, xb].astype(F32)
        if inner > 1:
            rx(b, c).wait_recv()
            value = value + xr[b, c].astype(F32)
        zb[b, c] = value.astype(BF16)
        for d in sorted(range(1, outer), key=lambda d: -min(d, outer - d)):
            to = lax.rem(za + d, outer)
            remote(
                zb.at[b, c, to], zr.at[b, c, d - 1], rz_send, rz_recv.at[b, c], at_z(to)
            ).start()

    def packing():
        r = lax.broadcasted_iota(jnp.int32, (each * TILE, parts * rows), 0)
        k = lax.broadcasted_iota(jnp.int32, (each * TILE, parts * rows), 1)
        col = (
            ((r & (TILE - 1)) >> log2(slots)) * rows
            + ((r >> log2(TILE)) << log2(slots)) + (r & (slots - 1))
        )
        return jnp.where(k == col, 1.0, 0.0).astype(BF16)

    def outer_sum(b, c):
        value = zb[b, c, za].astype(F32)
        if outer > 1:
            remote(zr.at[b, c], zr.at[b, c], rz_send, rz_recv.at[b, c], partner).wait_recv()
            for d in range(1, outer):
                value = value + zr[b, c, d - 1].astype(F32)
        unit, i = c // per, c % per
        summed[b, unit, i * tile_rows:(i + 1) * tile_rows] = value.astype(BF16)
        if i == per - 1:
            give(b, unit)

    def give(b, unit):
        back = jnp.dot(packing(), summed[b, unit], preferred_element_type=F32)
        rb[b, unit] = back.astype(BF16).reshape(each, TILE, wide)
        if b == 0:
            ob[unit, ex] = rb[b, unit, mine]
            ks = [lax.rem(mine + i, each) for i in range(1, each)]
        else:
            ks = list(range(each))
        for k in ks:
            j = lax.rem(chip * pair + b * each + k, ne)
            remote(rb.at[b, unit, k], ob.at[unit, ex], o_send, o_recv, (dp, j)).start()

    def weigh():
        get_gat.wait()
        terms = 3
        c_id = lax.broadcasted_iota(jnp.int32, (tokens_here, terms * packed), 1)
        n_id = lax.broadcasted_iota(jnp.int32, (tokens_here, terms * packed), 0)
        c_row = c_id & (packed - 1)
        c_slot = ((c_row >> log2(TILE)) << log2(slots)) + (c_row & (slots - 1))
        weight = jnp.zeros((tokens_here, terms * packed), F32)
        for e in range(ne):
            for s in range(slots):
                weight = jnp.where(
                    (c_slot == e * slots + s) & (n_id == sel[e, s]), gat[e, s], weight
                )
        left = weight
        coef = jnp.zeros_like(weight)
        for i in range(terms):
            term = left.astype(BF16).astype(F32)
            coef = jnp.where((c_id >> log2(packed)) == i, term, coef)
            left = left - term
        c_part = (c_row & (TILE - 1)) >> log2(slots)
        for p in range(parts):
            cmb[p] = jnp.where(c_part == p, coef, 0.0).astype(BF16)

    tasks = dict(
        first=own_first, own=own, arrive=arrive, relay=relay, distant=distant, spread=spread, ready=ready, mult=multiply,
        down=down, inner=inner_sum, outer=outer_sum, weigh=weigh,
    )
    for name, *args in order(batches, stages, blocks, chunks):
        with scope("_".join([name] + [str(a) for a in args])):
            tasks[name](*args)

    def drain(block, sem):
        remote(block, block, sem, sem, partner).wait_send()

    with scope("back"):
        landed = ob.at[:, 0:ne - 1]
        remote(landed, landed, o_send, o_recv, partner).wait_recv()
    drain(sb.at[:, 0:ne - 1], a_send)
    drain(landed, o_send)
    if outer > 1:
        drain(zb.at[:, :, 0:outer - 1], rz_send)
        for b in range(batches):
            relay = is_relayed(b, 0)
            drain(xp.at[b, :, 0, 0:half if relay else outer - 1], gz_send.at[b])
            if relay:
                @pl.when(za == near_gate)
                def _():
                    for i in range(half - 1):
                        drain(xp.at[b, :, 0, 0:half], gf_send.at[b, i])
    if inner > 1:
        drain(xp.at[:, :, 0], gx_send)
        drain(pb.at[:, :, 0], rx_send)


RELAY = (False, True)


def order(batches, stages, blocks, chunks):
    last = batches - 1
    both = range(batches)
    yield from (("first", q) for q in range(stages))
    yield ("spread",)
    for b in both:
        yield from (("own", b, q) for q in range(stages))
    for q in range(stages):
        yield ("arrive", 0, q)
        yield ("relay", 0, q)
        if last:
            yield ("arrive", 1, q)
    yield from (("distant", 0, q) for q in range(stages))
    yield ("weigh",)
    for q in range(stages):
        if last:
            yield ("relay", 1, q)
        yield ("ready", 0, q)
        for i in range(blocks):
            yield ("mult", 0, q, i)
            if last and q > 0 and i == 1:
                yield ("distant", 1, 0)
    for c in range(chunks):
        yield ("down", 0, c)
        if last and c < stages - 1:
            yield ("distant", 1, c + 1)
    n = 0
    if last:
        for q in range(stages):
            yield ("ready", 1, q)
            for i in range(blocks):
                yield ("mult", 1, q, i)
                if q > 0 and i % 2 == 1 and n < chunks:
                    yield ("inner", 0, n)
                    n += 1
        for c in range(chunks):
            yield ("down", 1, c)
            if c % 2 == 1 and n < chunks:
                yield ("inner", 0, n)
                n += 1
    for c in range(n, chunks):
        yield ("inner", 0, c)
    lag = 1
    for c in range(chunks + lag):
        if last and c < chunks:
            yield ("inner", 1, c)
        if c >= lag:
            yield ("outer", 0, c - lag)
    if last:
        yield from (("outer", 1, c) for c in range(chunks))


def mix(ob, cmb, out_hbm, out, sem):
    stages, ne, tile, wide = ob.shape
    parts, tokens_here, depth = cmb.shape
    packed = ne * tile
    terms = depth // packed
    span = parts * wide
    stores = []
    for q in range(stages):
        got = ob[q].reshape(packed, wide)
        total = jnp.dot(
            cmb[...].reshape(parts * tokens_here, depth),
            jnp.concatenate([got] * terms, axis=0),
            preferred_element_type=F32,
        ).astype(BF16)
        for p in range(parts):
            at = q * span + p * wide
            out[:, at:at + wide] = total[p * tokens_here:(p + 1) * tokens_here]
        at = pl.ds(q * span, span)
        store = pltpu.make_async_copy(out.at[:, at], out_hbm.at[:, at], sem.at[q])
        store.start()
        stores.append(store)
    for store in stores:
        store.wait()


def per_device(nd, ne, tokens, select, gates, w_gate, w_up, w_down):
    tok_dev, width = tokens.shape
    slots = select.shape[1]
    hidden = w_gate.shape[2]
    inner = 2 if nd % 2 == 0 else 1
    outer = nd // inner
    parts = TILE // slots
    batches = 2 if ne % 2 == 0 and (ne // 2 * slots) % 8 == 0 else 1
    each = ne // batches
    rows = each * slots
    stages = 2
    span = width // stages
    wide = span // parts
    fold = max(1, TILE // rows)
    tile_rows = fold * rows
    chunks = width // (fold * wide)
    total_rows = nd * rows
    vmem = pl.BlockSpec(memory_space=pltpu.VMEM)
    hbm = pl.BlockSpec(memory_space=pl.ANY)
    dma = pltpu.SemaphoreType.DMA
    returned, coef = pl.pallas_call(
        functools.partial(kernel, nd, ne),
        out_shape=(
            pltpu.VMEM((stages, ne, TILE, wide), BF16),
            pltpu.VMEM((parts, tok_dev, 3 * ne * TILE), BF16),
        ),
        in_specs=[hbm] * 6,
        out_specs=(vmem, vmem),
        scratch_shapes=[
            pltpu.VMEM((tok_dev, width), BF16),
            pltpu.SMEM(select.shape, jnp.int32),
            pltpu.SMEM(gates.shape, F32),
            pltpu.VMEM((width, hidden), BF16),
            pltpu.VMEM((width, hidden), BF16),
            pltpu.VMEM((hidden, width), BF16),
            pltpu.VMEM((stages, ne, TILE, wide), BF16),
            pltpu.VMEM((batches, stages, inner, outer, each, TILE, wide), BF16),
            pltpu.VMEM((parts * total_rows, parts * total_rows), BF16),
            pltpu.VMEM((total_rows, span), BF16),
            pltpu.VMEM((total_rows, hidden), F32),
            pltpu.VMEM((total_rows, hidden), F32),
            pltpu.VMEM((total_rows, hidden), BF16),
            pltpu.VMEM((batches, chunks, inner, outer, tile_rows, wide), BF16),
            pltpu.VMEM((batches, chunks, outer, tile_rows, wide), BF16),
            pltpu.VMEM((batches, chunks, outer, tile_rows, wide), BF16),
            pltpu.VMEM((batches, chunks, max(outer - 1, 1), tile_rows, wide), BF16),
            pltpu.VMEM((batches, stages, parts * rows, wide), BF16),
            pltpu.VMEM((batches, stages, each, TILE, wide), BF16),
            dma((3,)), dma((3,)),
            dma(()), dma((batches, stages)),
            dma((batches,)), dma((batches, max(outer // 2 - 1, 1))),
            dma((batches, stages, outer)),
            dma(()), dma((batches, stages)),
            dma(()), dma((batches, chunks)),
            dma(()), dma((batches, chunks)),
            dma(()), dma(()),
        ],
        compiler_params=pltpu.CompilerParams(
            collective_id=0, has_side_effects=True, vmem_limit_bytes=60 * 1024 * 1024
        ),
    )(tokens, select, gates, w_gate, w_up, w_down)
    return pl.pallas_call(
        mix,
        out_shape=jax.ShapeDtypeStruct((tok_dev, width), BF16),
        in_specs=[vmem, vmem],
        out_specs=hbm,
        scratch_shapes=[pltpu.VMEM((tok_dev, width), BF16), dma((stages,))],
    )(
        pltpu.with_memory_space_constraint(returned, pltpu.VMEM),
        pltpu.with_memory_space_constraint(coef, pltpu.VMEM),
    )


def solution(mesh):
    return jax.shard_map(
        functools.partial(per_device, mesh.shape["dp"], mesh.shape["expert"]),
        mesh=mesh,
        in_specs=(
            P(("dp", "expert"), None),
            P(None, ("dp", "expert")),
            P(None, ("dp", "expert")),
            P("expert", None, "dp"),
            P("expert", None, "dp"),
            P("expert", "dp", None),
        ),
        out_specs=P(("dp", "expert"), None),
        check_vma=False,
    )
```

time: 47 us -> 41.8 us (0.89)
  Pallas kernels: 46.8 us -> 41.7 us
    pallas_call x1, Pallas kernels: 45.5 us -> 40.4 us  [per_device(): pl.pallas_call(functools.partial(kernel, nd, ne), out_shape=(pltpu.VMEM((...]
where the time goes in v3:
time: 41.8 us; the launch traced here: 41.7 us
  Pallas kernels  41.7 us (100%)
    pallas_call x1, Pallas kernels, per_device(): pl.pallas_call(functools.partial(kernel, nd, ne), out_shape=(pltpu.VMEM((...  40.4 us
    pallas_call x1, Pallas kernels, per_device(): pl.pallas_call(mix, out_shape=jax.ShapeDtypeStruct((tok_dev, width), BF16...  1.27 us

profile of v3, /device:TPU:0, one launch (start us, length us, event | category | flops | bytes accessed | tf_op | source)
XLA Modules:
  0.0 41.7 jit_solution(18148653302193278101)
XLA Ops:
  0.0 40.4 %shard_map.64 = (bf16[2,4,16,512]{3,2,1,0:T(8,128)(2,1)S(1)}, bf16[4,128,192]{2,1,0:T(8,128)(2,1)S(1)}) custom-call(bf16[128,4096]{1,0:T(8,128)(2,1)} %tok_hbm.1, s32[4,4]{1,0:T(4,128)} %sel_hbm.1, f32[4,4]{1,0:T(4,128)} %gat_hbm.1, bf16[1,4096,1024]{2,1,0:T(8,128)(2,1)} %wg_hbm.1, bf16[1,4096,1024]{2,1,0:T(8,128)(2,1)} %wu_hbm.1, bf16[1,1024,4096]{2,1,0:T(8,128)(2,1)} %wd_hbm.1), custom_call_target="tpu_custom_call" | custom-call | tf_op jit(solution)/shard_map/pallas_call | solution.py:458
  40.4 1.3 %shard_map.65 = bf16[128,4096]{1,0:T(8,128)(2,1)} custom-call(bf16[2,4,16,512]{3,2,1,0:T(8,128)(2,1)S(1)} %get-tuple-element.7.ob, bf16[4,128,192]{2,1,0:T(8,128)(2,1)S(1)} %get-tuple-element.8.cmb), custom_call_target="tpu_custom_call" | custom-call | tf_op jit(solution)/shard_map/pallas_call | solution.py:499

commit v4 on v3

--- a/solution.py
+++ b/solution.py
@@ -127,26 +127,43 @@
                 sb.at[q, e], xp.at[b, q, xb, za, k], a_send, a_recv.at[b, q], (dp, e)
             ).start()
 
-    relayed = outer >= 4 and outer % 2 == 0
+    relayed = outer >= 4 and outer % 2 == 0 and pair > 1
     my_half = za // max(half, 1)
     near_gate = half - 1 + my_half
     far_gate = half - my_half
 
-    def is_relayed(b, q):
-        return relayed and RELAY[b]
-
-    def targets(b, q):
-        if not is_relayed(b, q):
-            return [lax.rem(za + d, outer) for d in sorted(range(1, outer), key=lambda d: min(d, outer - d))]
-        mates = [my_half * half + lax.rem(za - my_half * half + i, half) for i in range(1, half)]
-        return mates + [far_gate]
+    relays = core == pair - 1
+    near = sorted(range(1, outer), key=lambda d: min(d, outer - d))
+
+    def mate(i):
+        return my_half * half + lax.rem(za - my_half * half + i, half)
+
+    def far_side():
+        return [far_gate + i * (1 - 2 * my_half) for i in range(half)]
 
     def send_own(b, q, k, n):
         block = xp.at[b, q, xb, za, pl.ds(k, n)]
         if inner > 1:
             remote(block, block, gx_send, gx_recv.at[b, q], partner).start()
-        for z in targets(b, q):
+
+        def send(z):
             remote(block, block, gz_send.at[b], gz_recv.at[b, q, za], at_z(z)).start()
+
+        if not relayed:
+            for d in near:
+                send(lax.rem(za + d, outer))
+            return
+        for i in range(1, half):
+            send(mate(i))
+
+        @pl.when(relays)
+        def _():
+            send(far_gate)
+
+        @pl.when(jnp.logical_not(relays))
+        def _():
+            for z in far_side():
+                send(z)
 
     def own_first(q):
         send_own(0, q, mine, 1)
@@ -167,25 +184,19 @@
         if inner > 1:
             remote(block, block, gx_send, gx_recv.at[b, q], partner).start()
 
-    def mate(i):
-        return my_half * half + lax.rem(za - my_half * half + i, half)
-
     def arrive(b, q):
-        if not is_relayed(b, q):
-            for d in sorted(range(1, outer), key=lambda d: min(d, outer - d)):
+        if not relayed:
+            for d in near:
                 take(b, q, lax.rem(za + outer - d, outer))
             return
         for i in range(1, half):
             take(b, q, mate(i))
 
-    def far_side():
-        return [far_gate + i * (1 - 2 * my_half) for i in range(half)]
-
     def relay(b, q):
-        if not is_relayed(b, q):
+        if not relayed:
             return
 
-        @pl.when(za == near_gate)
+        @pl.when(relays & (za == near_gate))
         def _():
             for z in far_side():
                 take(b, q, z)
@@ -196,10 +207,10 @@
                     ).start()
 
     def distant(b, q):
-        if not is_relayed(b, q):
+        if not relayed:
             return
 
-        @pl.when(za != near_gate)
+        @pl.when(jnp.logical_not(relays & (za == near_gate)))
         def _():
             for z in far_side():
                 take(b, q, z)
@@ -263,10 +274,14 @@
             rx(b, c).wait_recv()
             value = value + xr[b, c].astype(F32)
         zb[b, c] = value.astype(BF16)
-        for d in sorted(range(1, outer), key=lambda d: -min(d, outer - d)):
-            to = lax.rem(za + d, outer)
+        if relayed:
+            order_z = far_side()[::-1] + [mate(i) for i in range(1, half)]
+        else:
+            order_z = [lax.rem(za + d, outer) for d in near[::-1]]
+        for to in order_z:
+            slot = lax.rem(to - za + outer, outer) - 1
             remote(
-                zb.at[b, c, to], zr.at[b, c, d - 1], rz_send, rz_recv.at[b, c], at_z(to)
+                zb.at[b, c, to], zr.at[b, c, slot], rz_send, rz_recv.at[b, c], at_z(to)
             ).start()
 
     def packing():
@@ -342,12 +357,23 @@
     drain(landed, o_send)
     if outer > 1:
         drain(zb.at[:, :, 0:outer - 1], rz_send)
-        for b in range(batches):
-            relay = is_relayed(b, 0)
-            drain(xp.at[b, :, 0, 0:half if relay else outer - 1], gz_send.at[b])
-            if relay:
-                @pl.when(za == near_gate)
-                def _():
+        if not relayed:
+            for b in range(batches):
+                drain(xp.at[b, :, 0, 0:outer - 1], gz_send.at[b])
+        else:
+            @pl.when(relays)
+            def _():
+                for b in range(batches):
+                    drain(xp.at[b, :, 0, 0:half], gz_send.at[b])
+
+            @pl.when(jnp.logical_not(relays))
+            def _():
+                for b in range(batches):
+                    drain(xp.at[b, :, 0, 0:outer - 1], gz_send.at[b])
+
+            @pl.when(relays & (za == near_gate))
+            def _():
+                for b in range(batches):
                     for i in range(half - 1):
                         drain(xp.at[b, :, 0, 0:half], gf_send.at[b, i])
     if inner > 1:
@@ -355,22 +381,21 @@
         drain(pb.at[:, :, 0], rx_send)
 
 
-RELAY = (False, True)
-
-
 def order(batches, stages, blocks, chunks):
     last = batches - 1
     both = range(batches)
-    yield from (("first", q) for q in range(stages))
+    for q in range(stages):
+        yield ("first", q)
+        yield ("own", 0, q)
     yield ("spread",)
-    for b in both:
-        yield from (("own", b, q) for q in range(stages))
+    if last:
+        yield from (("own", 1, q) for q in range(stages))
     for q in range(stages):
         yield ("arrive", 0, q)
         yield ("relay", 0, q)
-        if last:
-            yield ("arrive", 1, q)
     yield from (("distant", 0, q) for q in range(stages))
+    if last:
+        yield from (("arrive", 1, q) for q in range(stages))
     yield ("weigh",)
     for q in range(stages):
         if last:
@@ -378,18 +403,18 @@
         yield ("ready", 0, q)
         for i in range(blocks):
             yield ("mult", 0, q, i)
-            if last and q > 0 and i == 1:
-                yield ("distant", 1, 0)
-    for c in range(chunks):
-        yield ("down", 0, c)
-        if last and c < stages - 1:
-            yield ("distant", 1, c + 1)
+        if last:
+            yield ("distant", 1, q)
     n = 0
     if last:
+        yield ("down", 0, 0)
+        yield ("down", 0, 1)
         for q in range(stages):
             yield ("ready", 1, q)
             for i in range(blocks):
                 yield ("mult", 1, q, i)
+                if q == 0 and i % 2 == 1:
+                    yield ("down", 0, 2 + i // 2)
                 if q > 0 and i % 2 == 1 and n < chunks:
                     yield ("inner", 0, n)
                     n += 1

time: 41.8 us -> 41.2 us (0.986)
  Pallas kernels: 41.7 us -> 41.1 us
    pallas_call x1, Pallas kernels: 40.4 us -> 39.8 us  [per_device(): pl.pallas_call(functools.partial(kernel, nd, ne), out_shape=(pltpu.VMEM((...]
where the time goes in v4:
time: 41.2 us; the launch traced here: 41.1 us
  Pallas kernels  41.1 us (100%)
    pallas_call x1, Pallas kernels, per_device(): pl.pallas_call(functools.partial(kernel, nd, ne), out_shape=(pltpu.VMEM((...  39.8 us
    pallas_call x1, Pallas kernels, per_device(): pl.pallas_call(mix, out_shape=jax.ShapeDtypeStruct((tok_dev, width), BF16...  1.27 us

profile of v4, /device:TPU:0, one launch (start us, length us, event | category | flops | bytes accessed | tf_op | source)
XLA Modules:
  0.0 41.1 jit_solution(3946223429334199860)
XLA Ops:
  0.0 39.8 %shard_map.64 = (bf16[2,4,16,512]{3,2,1,0:T(8,128)(2,1)S(1)}, bf16[4,128,192]{2,1,0:T(8,128)(2,1)S(1)}) custom-call(bf16[128,4096]{1,0:T(8,128)(2,1)} %tok_hbm.1, s32[4,4]{1,0:T(4,128)} %sel_hbm.1, f32[4,4]{1,0:T(4,128)} %gat_hbm.1, bf16[1,4096,1024]{2,1,0:T(8,128)(2,1)} %wg_hbm.1, bf16[1,4096,1024]{2,1,0:T(8,128)(2,1)} %wu_hbm.1, bf16[1,1024,4096]{2,1,0:T(8,128)(2,1)} %wd_hbm.1), custom_call_target="tpu_custom_call" | custom-call | tf_op jit(solution)/shard_map/pallas_call | solution.py:483
  39.8 1.3 %shard_map.65 = bf16[128,4096]{1,0:T(8,128)(2,1)} custom-call(bf16[2,4,16,512]{3,2,1,0:T(8,128)(2,1)S(1)} %get-tuple-element.7.ob, bf16[4,128,192]{2,1,0:T(8,128)(2,1)S(1)} %get-tuple-element.8.cmb), custom_call_target="tpu_custom_call" | custom-call | tf_op jit(solution)/shard_map/pallas_call | solution.py:524

commit v5 on v4

--- a/solution.py
+++ b/solution.py
@@ -19,7 +19,7 @@
 
 
 def kernel(
-    nd, ne, tok_hbm, sel_hbm, gat_hbm, wg_hbm, wu_hbm, wd_hbm, ob, cmb,
+    nd, ne, tok_hbm, sel_hbm, gat_hbm, wg_hbm, wu_hbm, wd_hbm, ob, cmb, early,
     tok, sel, gat, wg, wu, wd, sb, xp, unp, xs, g_acc, u_acc, hid, pb, xr, zb, zr, summed, rb,
     l_sem, w_sem, a_send, a_recv, gz_send, gf_send, gz_recv, gx_send, gx_recv,
     rx_send, rx_recv, rz_send, rz_recv, o_send, o_recv,
@@ -314,7 +314,7 @@
             ks = list(range(each))
         for k in ks:
             j = lax.rem(chip * pair + b * each + k, ne)
-            remote(rb.at[b, unit, k], ob.at[unit, ex], o_send, o_recv, (dp, j)).start()
+            remote(rb.at[b, unit, k], ob.at[unit, ex], o_send, o_recv.at[unit], (dp, j)).start()
 
     def weigh():
         get_gat.wait()
@@ -350,9 +350,13 @@
     def drain(block, sem):
         remote(block, block, sem, sem, partner).wait_send()
 
-    with scope("back"):
-        landed = ob.at[:, 0:ne - 1]
-        remote(landed, landed, o_send, o_recv, partner).wait_recv()
+    for unit in range(units):
+        with scope("back"):
+            landed = ob.at[unit, 0:ne - 1]
+            remote(landed, landed, o_send, o_recv.at[unit], partner).wait_recv()
+        if unit < units - 1:
+            blend(ob, cmb, unit, early, unit * span)
+    landed = ob.at[:, 0:ne - 1]
     drain(sb.at[:, 0:ne - 1], a_send)
     drain(landed, o_send)
     if outer > 1:
@@ -435,29 +439,30 @@
         yield from (("outer", 1, c) for c in range(chunks))
 
 
-def mix(ob, cmb, out_hbm, out, sem):
-    stages, ne, tile, wide = ob.shape
+def blend(ob, cmb, unit, out, start):
+    _, ne, tile, wide = ob.shape
     parts, tokens_here, depth = cmb.shape
     packed = ne * tile
-    terms = depth // packed
-    span = parts * wide
-    stores = []
-    for q in range(stages):
-        got = ob[q].reshape(packed, wide)
-        total = jnp.dot(
-            cmb[...].reshape(parts * tokens_here, depth),
-            jnp.concatenate([got] * terms, axis=0),
-            preferred_element_type=F32,
-        ).astype(BF16)
-        for p in range(parts):
-            at = q * span + p * wide
-            out[:, at:at + wide] = total[p * tokens_here:(p + 1) * tokens_here]
-        at = pl.ds(q * span, span)
-        store = pltpu.make_async_copy(out.at[:, at], out_hbm.at[:, at], sem.at[q])
-        store.start()
-        stores.append(store)
-    for store in stores:
-        store.wait()
+    got = ob[unit].reshape(packed, wide)
+    total = jnp.dot(
+        cmb[...].reshape(parts * tokens_here, depth),
+        jnp.concatenate([got] * (depth // packed), axis=0),
+        preferred_element_type=F32,
+    ).astype(BF16)
+    for p in range(parts):
+        at = start + p * wide
+        out[:, at:at + wide] = total[p * tokens_here:(p + 1) * tokens_here]
+
+
+def mix(ob, cmb, early, out_hbm, late, sem):
+    done = early.shape[1]
+    first = pltpu.make_async_copy(early, out_hbm.at[:, pl.ds(0, done)], sem.at[0])
+    first.start()
+    blend(ob, cmb, ob.shape[0] - 1, late, 0)
+    second = pltpu.make_async_copy(late, out_hbm.at[:, pl.ds(done, late.shape[1])], sem.at[1])
+    second.start()
+    first.wait()
+    second.wait()
 
 
 def per_device(nd, ne, tokens, select, gates, w_gate, w_up, w_down):
@@ -480,14 +485,15 @@
     vmem = pl.BlockSpec(memory_space=pltpu.VMEM)
     hbm = pl.BlockSpec(memory_space=pl.ANY)
     dma = pltpu.SemaphoreType.DMA
-    returned, coef = pl.pallas_call(
+    handed = pl.pallas_call(
         functools.partial(kernel, nd, ne),
         out_shape=(
             pltpu.VMEM((stages, ne, TILE, wide), BF16),
             pltpu.VMEM((parts, tok_dev, 3 * ne * TILE), BF16),
+            pltpu.VMEM((tok_dev, width - span), BF16),
         ),
         in_specs=[hbm] * 6,
-        out_specs=(vmem, vmem),
+        out_specs=(vmem, vmem, vmem),
         scratch_shapes=[
             pltpu.VMEM((tok_dev, width), BF16),
             pltpu.SMEM(select.shape, jnp.int32),
@@ -515,7 +521,7 @@
             dma(()), dma((batches, stages)),
             dma(()), dma((batches, chunks)),
             dma(()), dma((batches, chunks)),
-            dma(()), dma(()),
+            dma(()), dma((stages,)),
         ],
         compiler_params=pltpu.CompilerParams(
             collective_id=0, has_side_effects=True, vmem_limit_bytes=60 * 1024 * 1024
@@ -524,13 +530,10 @@
     return pl.pallas_call(
         mix,
         out_shape=jax.ShapeDtypeStruct((tok_dev, width), BF16),
-        in_specs=[vmem, vmem],
+        in_specs=[vmem] * 3,
         out_specs=hbm,
-        scratch_shapes=[pltpu.VMEM((tok_dev, width), BF16), dma((stages,))],
-    )(
-        pltpu.with_memory_space_constraint(returned, pltpu.VMEM),
-        pltpu.with_memory_space_constraint(coef, pltpu.VMEM),
-    )
+        scratch_shapes=[pltpu.VMEM((tok_dev, span), BF16), dma((2,))],
+    )(*[pltpu.with_memory_space_constraint(array, pltpu.VMEM) for array in handed])
 
 
 def solution(mesh):

time: 41.2 us -> 41.1 us (level)
  no operation moved by 1% of the time
where the time goes in v5:
time: 41.1 us; the launch traced here: 40.9 us
  Pallas kernels  40.9 us (100%)
    pallas_call x1, Pallas kernels, per_device(): pl.pallas_call(functools.partial(kernel, nd, ne), out_shape=(pltpu.VMEM((...  39.8 us
    pallas_call x1, Pallas kernels, per_device(): pl.pallas_call(mix, out_shape=jax.ShapeDtypeStruct((tok_dev, width), BF16...  1.1 us

profile of v5, /device:TPU:0, one launch (start us, length us, event | category | flops | bytes accessed | tf_op | source)
XLA Modules:
  0.0 40.9 jit_solution(12966803746294323639)
XLA Ops:
  0.0 39.8 %shard_map.64 = (bf16[2,4,16,512]{3,2,1,0:T(8,128)(2,1)S(1)}, bf16[4,128,192]{2,1,0:T(8,128)(2,1)S(1)}, bf16[128,2048]{1,0:T(8,128)(2,1)S(1)}) custom-call(bf16[128,4096]{1,0:T(8,128)(2,1)} %tok_hbm.1, s32[4,4]{1,0:T(4,128)} %sel_hbm.1, f32[4,4]{1,0:T(4,128)} %gat_hbm.1, bf16[1,4096,1024]{2,1,0:T(8,128)(2,1)} %wg_hbm.1, bf16[1,4096,1024]{2,1,0:T(8,128)(2,1)} %wu_hbm.1, ...), custom_call_target="tpu_custom_call" | custom-call | tf_op jit(solution)/shard_map/pallas_call | solution.py:488
  39.8 1.1 %shard_map.65 = bf16[128,4096]{1,0:T(8,128)(2,1)} custom-call(bf16[2,4,16,512]{3,2,1,0:T(8,128)(2,1)S(1)} %get-tuple-element.8.ob, bf16[4,128,192]{2,1,0:T(8,128)(2,1)S(1)} %get-tuple-element.9.cmb, bf16[128,2048]{1,0:T(8,128)(2,1)S(1)} %get-tuple-element.10.early), custom_call_target="tpu_custom_call" | custom-call | tf_op jit(solution)/shard_map/pallas_call | solution.py:530
